TPU v7x, 768 devices: a whole 4x8x12 slice. The times are simulated.
768 devices in a mesh: fsdp: 64 (over x, y, core), blk: 12 (over z).
Axes of the slice: x: 4, y: 8, z: 12, core: 2. Of those that a mesh axis runs over, the one named last changes fastest.
Arguments:
- grad: bfloat16 [128, 768, 768], P(None, 'fsdp', 'blk'), may hold values from -16 to 16
- owner_slots: int32 [128], replicated, may hold values from 0 to 127, as said below
- stat_left: float32 [128, 768, 768], P('fsdp', None, 'blk'), may hold values from -6 to 6
- stat_right: float32 [128, 768, 768], P('fsdp', None, 'blk'), may hold values from -6 to 6
- basis_left: bfloat16 [128, 768, 768], P('fsdp'), may hold values from -1 to 1, as said below
- basis_right: bfloat16 [128, 768, 768], P('fsdp'), may hold values from -1 to 1, as said below
- moment: float32 [128, 768, 768], P('fsdp', None, 'blk'), may hold values from -3 to 3
- second: float32 [128, 768, 768], P('fsdp', None, 'blk'), may hold values from 0.01 to 0.1
Outputs:
- update: bfloat16 [128, 768, 768], P(None, 'fsdp', 'blk')
- new_left: float32 [128, 768, 768], P('fsdp', None, 'blk')
- new_right: float32 [128, 768, 768], P('fsdp', None, 'blk')
- new_moment: float32 [128, 768, 768], P('fsdp', None, 'blk')
- new_second: float32 [128, 768, 768], P('fsdp', None, 'blk')
- grad_rms: float32 [], replicated
Inputs may be any that keep to these rules, and one draw needn't show every extreme that they name: Each 768 x 768 block of basis_left is orthogonal up to bfloat16 rounding. Each 768 x 768 block of basis_right is orthogonal up to bfloat16 rounding. owner_slots names every block exactly once.
All inputs are finite; a program needn't handle non-finite values.
Results may differ from a plain program's by a relative error of at most 0.0058.
Values may be sent and summed in bfloat16 or wider, within the bound.
A program may use at most 64 MiB of HBM per device.

v0:
```python
import jax
import jax.numpy as jnp
from jax import lax
from jax.sharding import Mesh
from jax.sharding import PartitionSpec as P

BS = 768
FSDP = ("fsdp_0", "fsdp_1", "fsdp_2")
FSDP_BLK = ("fsdp_0", "fsdp_1", "fsdp_2", "blk")


clip_level = 0.5
stat_decay = 0.95
beta_one = 0.9
beta_two = 0.95
epsilon = 1e-08


def over_axes(shard, axes):
    for axis in axes:
        shard = lax.psum(shard, axis)
    return shard


def copy_for_each(shard, axis):
    copies = jnp.broadcast_to(shard, (lax.axis_size(axis), *shard.shape))
    return lax.all_to_all(copies, axis, split_axis=0, concat_axis=0, tiled=True)


def laid_out(blocks, dim):
    dims = list(blocks.shape[1:])
    dims[dim] *= blocks.shape[0]
    return jnp.moveaxis(blocks, 0, dim).reshape(dims)


def gather_directly(shard, axis, dim):
    blocks = copy_for_each(shard, axis)
    return laid_out(blocks, dim)


def body(grad, owner_slots, stat_left, stat_right, basis_left, basis_right, moment, second):
    arranged = jnp.take(grad, owner_slots, axis=0)
    owned = lax.all_to_all(arranged, FSDP, split_axis=0, concat_axis=1, tiled=True)
    width = owned.shape[2]
    first_col = lax.axis_index("blk") * width
    entries = grad.shape[0] * BS * BS
    partial_sum = jnp.sum(jnp.square(owned.astype(jnp.float32)))
    total = over_axes(partial_sum, FSDP_BLK)
    grad_rms = jnp.sqrt(total / entries)
    factor = jnp.minimum(1.0, clip_level / grad_rms)
    whole = lax.all_gather(owned, "blk", axis=2, tiled=True)
    own_rows = lax.dynamic_slice_in_dim(whole, first_col, width, 1)
    right_cols = lax.dynamic_slice_in_dim(basis_right, first_col, width, 2)
    outer_left = jnp.einsum("bij,bkj->bik", whole, own_rows, preferred_element_type=jnp.float32)
    outer_right = jnp.einsum("bji,bjk->bik", whole, owned, preferred_element_type=jnp.float32)
    new_left = stat_decay * stat_left + (1.0 - stat_decay) * (factor * factor) * outer_left
    new_right = stat_decay * stat_right + (1.0 - stat_decay) * (factor * factor) * outer_right
    turned = jnp.einsum(
        "bij,bjk->bik", whole, right_cols, preferred_element_type=jnp.float32
    ).astype(jnp.bfloat16)
    rotated = factor * jnp.einsum(
        "bji,bjk->bik", basis_left, turned, preferred_element_type=jnp.float32
    )
    new_moment = beta_one * moment + (1.0 - beta_one) * rotated
    new_second = beta_two * second + (1.0 - beta_two) * rotated * rotated
    scaled = (new_moment / (jnp.sqrt(new_second) + epsilon)).astype(jnp.bfloat16)
    back = jnp.einsum(
        "bij,bjk->bik", basis_left, scaled, preferred_element_type=jnp.float32
    ).astype(jnp.bfloat16)
    right_rows = lax.dynamic_slice_in_dim(basis_right, first_col, width, 1)
    summed = jnp.einsum(
        "bij,bkj->bik",
        gather_directly(back, "blk", 2),
        right_rows,
        preferred_element_type=jnp.float32,
    )
    stepped = summed.astype(jnp.bfloat16)
    returned = lax.all_to_all(stepped, FSDP, split_axis=1, concat_axis=0, tiled=True)
    placed = jnp.zeros_like(returned).at[owner_slots].set(returned)
    return (placed, new_left, new_right, new_moment, new_second, grad_rms)


def solution(mesh):
    torus = Mesh(
        mesh.devices.reshape(4, 8, 2, mesh.shape["blk"]), ("fsdp_0", "fsdp_1", "fsdp_2", "blk")
    )
    return jax.shard_map(
        body,
        mesh=torus,
        in_specs=(
            P(None, FSDP, "blk"),
            P(),
            P(FSDP, None, "blk"),
            P(FSDP, None, "blk"),
            P(FSDP, None, None),
            P(FSDP, None, None),
            P(FSDP, None, "blk"),
            P(FSDP, None, "blk"),
        ),
        out_specs=(
            P(None, FSDP, "blk"),
            P(FSDP, None, "blk"),
            P(FSDP, None, "blk"),
            P(FSDP, None, "blk"),
            P(FSDP, None, "blk"),
            P(),
        ),
        check_vma=False,
    )
```

profile of v0, /device:TPU:1, one launch (start us, length us, event | category | flops | bytes accessed | tf_op | source)
XLA Modules:
  0.0 227.3 jit_solution(7637785265295269094)
XLA Ops:
  7.2 0.0 copy-start
  7.2 0.0 all-gather.2.cloned.1.call-start
  7.2 0.8 compare_select_fusion
  8.0 0.7 compare_and_fusion
  8.7 1.4 copy.32
  10.1 0.7 gather_fusion
  10.8 0.2 broadcast_select_fusion
  11.0 0.3 reshape.39
  11.3 24.8 %all_to_all.41 = bf16[64,2,768]{2,1,0:T(2,128)(2,1)S(1)} all-to-all(bf16[64,2,768]{2,1,0:T(2,128)(2,1)S(1)} %reshape.39), channel_id=1, replica_groups=mesh['fsdp_0'=4,'fsdp_1'=8,'fsdp_2'=2,'blk'=12] {'fsdp_0','fsdp_1','fsdp..., dimensions={0} | all-to-all | bytes 393216 | tf_op jit(solution)/shard_map/all_to_all | solution.py:43
  36.0 0.3 reshape.40
  36.3 0.1 copy.33
  36.4 0.3 copy.34
  36.7 1.0 copy.35
  37.7 0.0 all-gather.2.cloned.1.call-update
  37.8 1.4 multiply_reduce_fusion
  39.2 8.6 %psum.28 = f32[]{:T(128)} all-reduce(f32[]{:T(128)} %multiply_reduce_fusion), channel_id=1, replica_groups=mesh['fsdp_0'=4,'fsdp_1'=8,'fsdp_2'=2,'blk'=12] {'fsdp_0'}, use_global_device_ids=true, to_apply=%region_1.2 | all-reduce | flops 1 | bytes 8 | tf_op jit(solution)/shard_map/psum | solution.py:21
  47.8 11.7 %psum.29 = f32[]{:T(128)} all-reduce(f32[]{:T(128)} %psum.28), channel_id=1, replica_groups=mesh['fsdp_0'=4,'fsdp_1'=8,'fsdp_2'=2,'blk'=12] {'fsdp_1'}, use_global_device_ids=true, to_apply=%region_2.3 | all-reduce | flops 1 | bytes 8 | tf_op jit(solution)/shard_map/psum | solution.py:21
  59.5 8.9 %psum.30 = f32[]{:T(128)} all-reduce(f32[]{:T(128)} %psum.29), channel_id=1, replica_groups=mesh['fsdp_0'=4,'fsdp_1'=8,'fsdp_2'=2,'blk'=12] {'fsdp_2'}, use_global_device_ids=true, to_apply=%region_3.4 | all-reduce | flops 1 | bytes 8 | tf_op jit(solution)/shard_map/psum | solution.py:21
  68.5 27.3 %psum.31 = f32[]{:T(128)} all-reduce(f32[]{:T(128)} %psum.30), channel_id=1, replica_groups=mesh['fsdp_0'=4,'fsdp_1'=8,'fsdp_2'=2,'blk'=12] {'blk'}, use_global_device_ids=true, to_apply=%region_4.5 | all-reduce | flops 1 | bytes 8 | tf_op jit(solution)/shard_map/psum | solution.py:21
  96.5 0.0 all-gather.2.cloned.1.call-done
  96.6 0.0 copy-done
  96.6 3.0 %fusion.25 = (f32[2,768,64]{1,2,0:T(8,128)S(1)}, f32[2,768,64]{1,2,0:T(8,128)S(1)}) fusion(f32[2,768,64]{1,2,0:T(8,128)} %param.15, f32[2,768,64]{1,2,0:T(8,128)} %param.14, bf16[2,768,768]{2,1,0:T(8,128)(2,1)S(1)} %copy-done, bf16[2,768,768]{1,0,2:T(2,128)(2,1)} %all-gather.2.cloned.1.call-done, bf16[2,768,768]{2,1,0:T(8,128)(2,1)} %param.13, ...), kind=kOutput, calls=%fused_computation.21 | convolution fusion | flops 302874624 | bytes 6684680 | tf_op jit(solution)/shard_map/bji,bjk->bik/dot_general | solution.py:61
  99.6 0.0 copy-start.1
  99.6 0.0 copy-start.2
  99.6 0.8 fusion.22
  100.5 1.7 broadcast_in_dim.23
  102.2 0.0 copy-done.1
  102.2 0.0 copy-done.2
  102.2 4.5 %all-to-all-start.1 = ((bf16[12,2,768,64]{2,3,1,0:T(8,128)(2,1)}), bf16[12,2,768,64]{2,3,1,0:T(8,128)(2,1)}, u32[]{:S(2)}, u32[]{:S(2)}) async-start(bf16[12,2,768,64]{2,3,1,0:T(8,128)(2,1)} %broadcast_in_dim.23), calls=%async_computation.1 | async-start | bytes 4718592 | tf_op jit(solution)/shard_map/all_to_all | solution.py:27
  106.6 3.3 %fusion.13 = f32[2,768,64]{1,2,0:T(8,128)} fusion(bf16[2,768,768]{1,0,2:T(2,128)(2,1)} %all-gather.2.cloned.1.call-done, bf16[2,768,64]{2,0,1:T(2,128)(2,1)S(1)} %bitcast.25, f32[2,768,64]{1,2,0:T(8,128)} %param.11, f32[]{:T(128)S(6)} %mul.74), kind=kOutput, calls=%fused_computation.12 | convolution fusion | flops 151289856 | bytes 3342340 | tf_op jit(solution)/shard_map/bji,bjk->bik/dot_general | solution.py:55
  109.9 66.0 %all-to-all-done.1 = bf16[12,2,768,64]{2,3,1,0:T(8,128)(2,1)} async-done(((bf16[12,2,768,64]{2,3,1,0:T(8,128)(2,1)}), bf16[12,2,768,64]{2,3,1,0:T(8,128)(2,1)}, u32[]{:S(2)}, u32[]{:S(2)}) %all-to-all-start.1) | async-done | bytes 2359328 | tf_op jit(solution)/shard_map/all_to_all | solution.py:27
  175.9 1.9 copy.38
  177.8 0.0 copy-start.3
  177.8 1.5 convolution_convert_fusion
  179.3 0.4 copy.40
  179.8 0.9 reshape.41
  180.7 21.2 %all-to-all-start.2 = ((bf16[64,2,768]{2,1,0:T(2,128)(2,1)}), bf16[64,2,768]{2,1,0:T(2,128)(2,1)S(1)}, u32[]{:S(2)}, u32[]{:S(2)}) async-start(bf16[64,2,768]{2,1,0:T(2,128)(2,1)} %reshape.41), calls=%async_computation.2 | async-start | bytes 393216 | tf_op jit(solution)/shard_map/all_to_all | solution.py:78
  201.9 1.5 constant_dynamic-slice_fusion
  203.4 0.0 copy-done.3
  203.4 3.0 %fusion.16 = f32[2,768,64]{1,2,0:T(8,128)} fusion(bf16[2,768,768]{1,0,2:T(2,128)(2,1)} %all-gather.2.cloned.1.call-done, bf16[2,64,768]{1,0,2:T(2,128)(2,1)S(1)} %constant_dynamic-slice_fusion, f32[2,768,64]{1,2,0:T(8,128)S(1)} %copy-done.3, f32[]{:T(128)S(6)} %mul.74), kind=kOutput, calls=%fused_computation.13 | convolution fusion | flops 151289856 | bytes 3342340 | tf_op jit(solution)/shard_map/bij,bkj->bik/dot_general | solution.py:54
  206.4 6.4 %all-to-all-done.2 = bf16[64,2,768]{2,1,0:T(2,128)(2,1)S(1)} async-done(((bf16[64,2,768]{2,1,0:T(2,128)(2,1)}), bf16[64,2,768]{2,1,0:T(2,128)(2,1)S(1)}, u32[]{:S(2)}, u32[]{:S(2)}) %all-to-all-start.2) | async-done | bytes 196640 | tf_op jit(solution)/shard_map/all_to_all | solution.py:78
  212.8 0.3 reshape.42
  213.1 0.3 copy.41
  213.5 0.3 copy.42
  213.8 0.1 broadcast_in_dim.19
  213.8 4.4 %scatter_fusion = bf16[128,12,64]{2,1,0:T(8,128)(2,1)S(1)} fusion(bf16[128,12,64]{2,1,0:T(8,128)(2,1)S(1)} %broadcast_in_dim.19, s32[128]{0:T(128)S(1)} %compare_select_fusion, bf16[128,12,64]{2,1,0:T(8,128)(2,1)S(1)} %copy.42), kind=kCustom, calls=%fused_computation.1 | custom fusion | bytes 590336 | tf_op jit(solution)/shard_map/scatter | solution.py:79
  218.3 1.0 copy.47
  (1 shorter events, 0.0 us)
Async XLA Ops:
  7.2 89.4 %copy-start = (bf16[2,768,768]{2,1,0:T(8,128)(2,1)S(1)}, bf16[2,768,768]{2,1,0:T(8,128)(2,1)}, u32[]{:S(2)}) copy-start(bf16[2,768,768]{2,1,0:T(8,128)(2,1)} %param.12) | copy-start | bytes 7077892
  7.2 89.4 %all-gather.2.cloned.1.call-start = ((), (), s32[]{:S(2)}) async-start(), calls=%async_computation.3 | async-start | bytes 2555904 | tf_op jit(solution)/shard_map/all_gather | solution.py:51
  99.6 2.6 %copy-start.1 = (f32[2,768,64]{1,2,0:T(8,128)}, f32[2,768,64]{1,2,0:T(8,128)S(1)}, u32[]{:S(2)}) copy-start(f32[2,768,64]{1,2,0:T(8,128)S(1)} %get-tuple-element.18) | copy-start | bytes 1179652
  99.6 2.6 %copy-start.2 = (f32[2,768,64]{1,2,0:T(8,128)}, f32[2,768,64]{1,2,0:T(8,128)S(1)}, u32[]{:S(2)}) copy-start(f32[2,768,64]{1,2,0:T(8,128)S(1)} %get-tuple-element.19) | copy-start | bytes 1179652
  102.2 73.7 %all-to-all-start.1 = ((bf16[12,2,768,64]{2,3,1,0:T(8,128)(2,1)}), bf16[12,2,768,64]{2,3,1,0:T(8,128)(2,1)}, u32[]{:S(2)}, u32[]{:S(2)}) async-start(bf16[12,2,768,64]{2,3,1,0:T(8,128)(2,1)} %broadcast_in_dim.23), calls=%async_computation.1 | async-start | bytes 4718592 | tf_op jit(solution)/shard_map/all_to_all | solution.py:27
  177.8 25.6 %copy-start.3 = (f32[2,768,64]{1,2,0:T(8,128)S(1)}, f32[2,768,64]{1,2,0:T(8,128)}, u32[]{:S(2)}) copy-start(f32[2,768,64]{1,2,0:T(8,128)} %param.10) | copy-start | bytes 1179652
  180.7 32.2 %all-to-all-start.2 = ((bf16[64,2,768]{2,1,0:T(2,128)(2,1)}), bf16[64,2,768]{2,1,0:T(2,128)(2,1)S(1)}, u32[]{:S(2)}, u32[]{:S(2)}) async-start(bf16[64,2,768]{2,1,0:T(2,128)(2,1)} %reshape.41), calls=%async_computation.2 | async-start | bytes 393216 | tf_op jit(solution)/shard_map/all_to_all | solution.py:78
Sparse Core Ops, SparseCore 0:
  37.9 54.3 all-gather.1
where the time goes:
time: 228 us; the launch traced here: 227 us
  blocking collectives  81.4 us (36%)
  waiting for transfers between devices  72.5 us (32%)
  starting transfers between devices  25.7 us (11%)
  local copies, waits for them, and re-layouts  16.9 us (7%)
  between operations  16.1 us (7%)
  matrix products  11.7 us (5%)
  other arithmetic  3.09 us (1%)
    all_to_all x1, waiting for transfers between devices, copy_for_each(): return lax.all_to_all(copies, axis, split_axis=0, concat_axis=0, tiled=True)  66 us
    psum x4, blocking collectives, over_axes(): shard = lax.psum(shard, axis)  56.6 us
    all_to_all x1, blocking collectives, body(): lax.all_to_all(arranged, FSDP, split_axis=0, concat_axis=1, tiled=True)  24.8 us
    all_to_all x1, starting transfers between devices, body(): lax.all_to_all(stepped, FSDP, split_axis=1, concat_axis=0, tiled=True)  21.2 us
    all_to_all x1, waiting for transfers between devices, body(): lax.all_to_all(stepped, FSDP, split_axis=1, concat_axis=0, tiled=True)  6.45 us
  transfers between devices with their start and end apart: 3, of which 2 were waited for; matrix products, arithmetic and copies ran while one was open for 4% of the time, Pallas kernels for 0%

commit v1 on v0

v1 whole, which is shorter than its diff:
```python
import functools

import jax
import jax.numpy as jnp
from jax import lax
from jax.experimental import pallas as pl
from jax.experimental.pallas import tpu as pltpu
from jax.sharding import PartitionSpec as P

BS = 768
NF = 64
NZ = 12
ROWS = BS // NF
PAD = 16
COLS = BS // NZ
LANES = 128
PER = BS // LANES
SLOTS = 2
PIECES = 2
PIECE = COLS // PIECES

clip_level = 0.5
stat_decay = 0.95
beta_one = 0.9
beta_two = 0.95
epsilon = 1e-08

F32 = jnp.float32
BF16 = jnp.bfloat16


def nn(a, b):
    return lax.dot_general(a, b, (((1,), (0,)), ((), ())), preferred_element_type=F32)


def nt(a, b):
    return lax.dot_general(a, b, (((1,), (1,)), ((), ())), preferred_element_type=F32)


def tn(a, b):
    return lax.dot_general(a, b, (((0,), (0,)), ((), ())), preferred_element_type=F32)


def kernel(
    entries,
    a_hbm,
    ql_hbm,
    qr_hbm,
    left_hbm,
    right_hbm,
    moment_hbm,
    second_hbm,
    w_out,
    left_out,
    right_out,
    moment_out,
    second_out,
    rms_out,
    a_ref,
    x_ref,
    gt_ref,
    ql_ref,
    qr_ref,
    state_ref,
    spread_ref,
    pick_ref,
    cols_ref,
    part_ref,
    plane_parts,
    plane_ref,
    all_parts,
    bt_ref,
    b_ref,
    ut_ref,
    ur_ref,
    u2_ref,
    y_ref,
    w_ref,
    load_sem,
    store_sem,
    x_send,
    x_recv,
    ring_send,
    ring_recv,
    part_send,
    part_recv,
    all_send,
    all_recv,
    b_send,
    b_recv,
    u_send,
    u_recv,
    w_send,
    w_recv,
):
    f = lax.axis_index("fsdp")
    z = lax.axis_index("blk")

    def along_f(step):
        return lax.rem(f + step, NF)

    def along_z(step):
        return lax.rem(z + step, NZ)

    x_ref[...] = jnp.zeros_like(x_ref)

    barrier = pltpu.get_barrier_semaphore()

    def greet_f(step, _):
        pl.semaphore_signal(barrier, inc=1, device_id={"fsdp": along_f(step)}, device_id_type=pl.DeviceIdType.MESH)
        return 0

    def greet_z(step, _):
        pl.semaphore_signal(barrier, inc=1, device_id={"blk": along_z(step)}, device_id_type=pl.DeviceIdType.MESH)
        return 0

    lax.fori_loop(1, NF, greet_f, 0)
    lax.fori_loop(1, NZ, greet_z, 0)

    loads = [
        pltpu.make_async_copy(qr_hbm, qr_ref, load_sem.at[0]),
        pltpu.make_async_copy(ql_hbm, ql_ref, load_sem.at[1]),
        pltpu.make_async_copy(moment_hbm, state_ref.at[0], load_sem.at[2]),
        pltpu.make_async_copy(second_hbm, state_ref.at[1], load_sem.at[3]),
        pltpu.make_async_copy(left_hbm, state_ref.at[2], load_sem.at[4]),
        pltpu.make_async_copy(right_hbm, state_ref.at[3], load_sem.at[5]),
        pltpu.make_async_copy(a_hbm, a_ref, load_sem.at[6]),
    ]
    for load in loads[::-1]:
        load.start()

    q = lax.broadcasted_iota(jnp.int32, spread_ref.shape, 0)
    r = lax.broadcasted_iota(jnp.int32, spread_ref.shape, 1)
    group = q // PAD
    inside = q - group * PAD
    spread_ref[...] = jnp.where((inside < ROWS) & (r == group * ROWS + inside), 1.0, 0.0).astype(BF16)
    k = lax.broadcasted_iota(jnp.int32, pick_ref.shape, 0)
    r = lax.broadcasted_iota(jnp.int32, pick_ref.shape, 1)
    pick_ref[...] = jnp.where(r == z * COLS + k, 1.0, 0.0).astype(BF16)

    loads[6].wait()
    pl.semaphore_wait(barrier, NF - 1 + NZ - 1)

    def exchange_f(src, dst, send, recv, step, src_at=None):
        to = along_f(step)
        return pltpu.make_async_remote_copy(
            src_ref=src if src_at is None else src.at[to, pl.ds(0, ROWS)],
            dst_ref=dst.at[f] if src_at is None else dst.at[f, pl.ds(0, ROWS)],
            send_sem=send.at[0],
            recv_sem=recv.at[0],
            device_id={"fsdp": to},
            device_id_type=pl.DeviceIdType.MESH,
        )

    def exchange_z(src, dst, send, recv, step, src_at=None):
        to = along_z(step)
        return pltpu.make_async_remote_copy(
            src_ref=src if src_at is None else src.at[to],
            dst_ref=dst.at[z],
            send_sem=send.at[0],
            recv_sem=recv.at[0],
            device_id={"blk": to},
            device_id_type=pl.DeviceIdType.MESH,
        )

    def send_all(exchange, count, *refs, **kw):
        def one(step, _):
            exchange(*refs, step, **kw).start()
            return 0

        lax.fori_loop(1, count, one, 0)

    def all_of(ref, count, send, recv, axis, rows=None):
        some = ref.at[pl.ds(0, count - 1)] if rows is None else ref.at[pl.ds(0, count - 1), pl.ds(0, rows)]
        return pltpu.make_async_remote_copy(
            src_ref=some,
            dst_ref=some,
            send_sem=send.at[0],
            recv_sem=recv.at[0],
            device_id={axis: along_f(1) if axis == "fsdp" else along_z(1)},
            device_id_type=pl.DeviceIdType.MESH,
        )

    send_all(exchange_f, NF, a_ref, x_ref, x_send, x_recv, src_at=True)
    x_ref[f, pl.ds(0, ROWS)] = a_ref[f]
    x_all = all_of(x_ref, NF, x_send, x_recv, "fsdp", ROWS)

    loads[0].wait()
    for s in range(SLOTS):
        cols_ref[s] = nt(pick_ref[...], qr_ref[s]).astype(BF16)

    x_all.wait_recv()
    half = NF // 2 * PAD
    wide = BS // 2
    for g in range(2):
        block = x_ref[pl.ds(g * (NF // 2), NF // 2)].reshape(half, LANES)
        panel = tn(block, spread_ref[...]).astype(BF16)
        for s in range(SLOTS):
            gt_ref[s, z, :, pl.ds(g * wide, wide)] = panel[s * COLS : (s + 1) * COLS]
    values = x_ref[...].astype(F32)
    part_ref[...] = jnp.full(part_ref.shape, jnp.sum(values * values), F32)

    hops = {}
    streams = [(s, way, p) for p in range(PIECES) for s in range(SLOTS) for way in range(2)]
    for s, way, p in streams:
        last = NZ // 2 if s == way else NZ // 2 - 1
        for t in range(last):
            origin = along_z(NZ - t) if way == 0 else along_z(t)
            to = along_z(1) if way == 0 else along_z(NZ - 1)
            hops[s, way, p, t] = pltpu.make_async_remote_copy(
                src_ref=gt_ref.at[s, origin, pl.ds(p * PIECE, PIECE)],
                dst_ref=gt_ref.at[s, origin, pl.ds(p * PIECE, PIECE)],
                send_sem=ring_send.at[s, way, p, t],
                recv_sem=ring_recv.at[s, way, p, t],
                device_id={"blk": to},
                device_id_type=pl.DeviceIdType.MESH,
            )

    for t in range(NZ // 2):
        for s, way, p in streams:
            if (s, way, p, t - 1) in hops:
                hops[s, way, p, t - 1].wait_recv()
            if (s, way, p, t) in hops:
                hops[s, way, p, t].start()
        if t == 0:
            send_all(exchange_f, NF, part_ref, plane_parts, part_send, part_recv)
            plane_parts[f] = part_ref[...]
        if t == 2:
            plane_all = all_of(plane_parts, NF, part_send, part_recv, "fsdp")
            plane_all.wait_recv()
            plane_ref[...] = jnp.sum(plane_parts[...], axis=0)
            send_all(exchange_z, NZ, plane_ref, all_parts, all_send, all_recv)
            all_parts[z] = plane_ref[...]
        if t == 4:
            all_all = all_of(all_parts, NZ, all_send, all_recv, "blk")
            all_all.wait_recv()
            total = jnp.sum(all_parts[...], axis=0)
            grad_rms = jnp.sqrt(total / entries)
            rms_out[...] = grad_rms
            part = jnp.minimum(1.0, clip_level / grad_rms)
            factor = jnp.broadcast_to(part[0:1, 0:1], (COLS, BS))
    for load in loads[1:6]:
        load.wait()
    for s, way, p in streams:
        if s == way:
            hops[s, way, p, NZ // 2 - 1].wait_recv()

    stores = []
    for s in range(SLOTS):
        gt = gt_ref[s].reshape(BS, BS)
        turned = nn(cols_ref[s], gt).astype(BF16)
        rotated = factor * nn(turned, ql_ref[s])
        new_moment = beta_one * state_ref[0, s] + (1.0 - beta_one) * rotated
        new_second = beta_two * state_ref[1, s] + (1.0 - beta_two) * rotated * rotated
        state_ref[0, s] = new_moment
        state_ref[1, s] = new_second
        scaled = (new_moment / (jnp.sqrt(new_second) + epsilon)).astype(BF16)
        back = nt(scaled, ql_ref[s]).astype(BF16)
        for j in range(PER):
            bt_ref[s * PER + j] = back[:, j * LANES : (j + 1) * LANES]

    send_all(exchange_z, NZ, bt_ref, b_ref, b_send, b_recv, src_at=True)
    b_ref[z] = bt_ref[z]
    stores.append(pltpu.make_async_copy(state_ref.at[0], moment_out, store_sem.at[0]))
    stores.append(pltpu.make_async_copy(state_ref.at[1], second_out, store_sem.at[1]))
    for store in stores:
        store.start()
    weight = (1.0 - stat_decay) * (factor * factor)
    for s in range(SLOTS):
        gt = gt_ref[s].reshape(BS, BS)
        rows = nt(pick_ref[...], gt).astype(BF16)
        state_ref[2, s] = stat_decay * state_ref[2, s] + weight * nn(rows, gt)
    stores.append(pltpu.make_async_copy(state_ref.at[2], left_out, store_sem.at[2]))
    stores[-1].start()

    b_all = all_of(b_ref, NZ, b_send, b_recv, "blk")
    b_all.wait_recv()
    stepped = nn(qr_ref[z // PER], b_ref[...].reshape(BS, LANES)).astype(BF16)
    ut_ref[...] = stepped.reshape(NZ, COLS, LANES)

    send_all(exchange_z, NZ, ut_ref, ur_ref, u_send, u_recv, src_at=True)
    ur_ref[z] = ut_ref[z]
    for s in range(SLOTS):
        gt = gt_ref[s].reshape(BS, BS)
        state_ref[3, s] = stat_decay * state_ref[3, s] + weight * nt(gt_ref[s, z], gt)
    stores.append(pltpu.make_async_copy(state_ref.at[3], right_out, store_sem.at[3]))
    stores[-1].start()

    u_all = all_of(ur_ref, NZ, u_send, u_recv, "blk")
    u_all.wait_recv()
    for s in range(SLOTS):
        for j in range(PER):
            u2_ref[pl.ds(s * COLS, COLS), pl.ds(j * LANES, LANES)] = ur_ref[s * PER + j]
    for g in range(2):
        rows = nt(spread_ref[...], u2_ref[:, pl.ds(g * wide, wide)]).astype(BF16)
        y_ref[pl.ds(g * (NF // 2), NF // 2)] = rows.reshape(NF // 2, PAD, LANES)

    send_all(exchange_f, NF, y_ref, w_ref, w_send, w_recv, src_at=True)
    w_ref[f, pl.ds(0, ROWS)] = y_ref[f, pl.ds(0, ROWS)]
    w_all = all_of(w_ref, NF, w_send, w_recv, "fsdp", ROWS)
    w_all.wait_recv()
    w_out[...] = w_ref[:, pl.ds(0, ROWS)]

    x_all.wait_send()
    plane_all.wait_send()
    all_all.wait_send()
    for hop in hops.values():
        hop.wait_send()
    b_all.wait_send()
    u_all.wait_send()
    w_all.wait_send()
    for store in stores:
        store.wait()


def body(grad, owner_slots, stat_left, stat_right, basis_left, basis_right, moment, second):
    blocks = grad.shape[0]
    chosen = (owner_slots[:, None] == jnp.arange(blocks, dtype=jnp.int32)[None, :]).astype(BF16)
    arranged = jnp.einsum("tb,brc->trc", chosen, grad, preferred_element_type=BF16)
    arranged = arranged.reshape(NF, SLOTS, ROWS, COLS).transpose(0, 2, 1, 3).reshape(NF, ROWS, LANES)

    state = jax.ShapeDtypeStruct((SLOTS, COLS, BS), F32)
    vmem = pl.BlockSpec(memory_space=pltpu.VMEM)
    any_ = pl.BlockSpec(memory_space=pl.ANY)
    dma = pltpu.SemaphoreType.DMA
    returned, new_left, new_right, new_moment, new_second, rms = pl.pallas_call(
        functools.partial(kernel, float(blocks * BS * BS)),
        out_shape=(
            jax.ShapeDtypeStruct((NF, ROWS, LANES), BF16),
            state,
            state,
            state,
            state,
            jax.ShapeDtypeStruct((8, LANES), F32),
        ),
        in_specs=[any_] * 7,
        out_specs=(vmem, any_, any_, any_, any_, vmem),
        scratch_shapes=[
            pltpu.VMEM((NF, ROWS, LANES), BF16),
            pltpu.VMEM((NF, PAD, LANES), BF16),
            pltpu.VMEM((SLOTS, NZ, COLS, BS), BF16),
            pltpu.VMEM((SLOTS, BS, BS), BF16),
            pltpu.VMEM((SLOTS, BS, BS), BF16),
            pltpu.VMEM((4, SLOTS, COLS, BS), F32),
            pltpu.VMEM((NF // 2 * PAD, BS // 2), BF16),
            pltpu.VMEM((COLS, BS), BF16),
            pltpu.VMEM((SLOTS, COLS, BS), BF16),
            pltpu.VMEM((8, LANES), F32),
            pltpu.VMEM((NF, 8, LANES), F32),
            pltpu.VMEM((8, LANES), F32),
            pltpu.VMEM((NZ, 8, LANES), F32),
            pltpu.VMEM((NZ, COLS, LANES), BF16),
            pltpu.VMEM((NZ, COLS, LANES), BF16),
            pltpu.VMEM((NZ, COLS, LANES), BF16),
            pltpu.VMEM((NZ, COLS, LANES), BF16),
            pltpu.VMEM((SLOTS * COLS, BS), BF16),
            pltpu.VMEM((NF, PAD, LANES), BF16),
            pltpu.VMEM((NF, PAD, LANES), BF16),
            dma((7,)),
            dma((4,)),
            dma((1,)),
            dma((1,)),
            dma((SLOTS, 2, PIECES, NZ // 2)),
            dma((SLOTS, 2, PIECES, NZ // 2)),
        ]
        + [dma((1,))] * 10,
        compiler_params=pltpu.CompilerParams(collective_id=0, has_side_effects=True),
    )(
        arranged,
        basis_left,
        basis_right,
        stat_left.swapaxes(1, 2),
        stat_right.swapaxes(1, 2),
        moment.swapaxes(1, 2),
        second.swapaxes(1, 2),
    )
    returned = returned.reshape(NF, ROWS, SLOTS, COLS).transpose(0, 2, 1, 3)
    returned = returned.reshape(blocks, ROWS, COLS)
    placed = jnp.einsum("tb,trc->brc", chosen, returned, preferred_element_type=BF16)
    return (
        placed,
        new_left.swapaxes(1, 2),
        new_right.swapaxes(1, 2),
        new_moment.swapaxes(1, 2),
        new_second.swapaxes(1, 2),
        rms[0, 0],
    )


def solution(mesh):
    rows = P(None, "fsdp", "blk")
    held = P("fsdp", None, "blk")
    whole = P("fsdp", None, None)
    return jax.shard_map(
        body,
        mesh=mesh,
        in_specs=(rows, P(), held, held, whole, whole, held, held),
        out_specs=(rows, held, held, held, held, P()),
        check_vma=False,
    )
```

time: 228 us -> 98.9 us (0.43)
  Pallas kernels: 0 us -> 87.8 us
  blocking collectives: 81.4 us -> 0 us
  waiting for transfers between devices: 72.5 us -> 0 us
  starting transfers between devices: 25.7 us -> 0 us
  between operations: 16.1 us -> 0.74 us
  matrix products: 11.7 us -> 1.88 us
  local copies, waits for them, and re-layouts: 16.9 us -> 8.17 us
  other arithmetic: 3.09 us -> 0.16 us
    pallas_call x0 -> x1, Pallas kernels: none -> 87.8 us  [body(): pl.pallas_call(functools.partial(kernel, float(blocks * BS * BS)), out_sh...]
    all_to_all x2 -> x0, waiting for transfers between devices: 72.4 us -> none  [the longest x1 66 us: copy_for_each(): return lax.all_to_all(copies, axis, split_axis=0, concat_axis=0, tiled=True)]
    psum x4 -> x0, blocking collectives: 56.6 us -> none  [over_axes(): shard = lax.psum(shard, axis)]
    all_to_all x2 -> x0, starting transfers between devices: 25.7 us -> none  [the longest x1 21.2 us: body(): lax.all_to_all(stepped, FSDP, split_axis=1, concat_axis=0, tiled=True)]
    all_to_all x1 -> x0, blocking collectives: 24.8 us -> none  [body(): lax.all_to_all(arranged, FSDP, split_axis=0, concat_axis=1, tiled=True)]
    dot_general x5 -> x0, matrix products: 11.7 us -> none  [the longest x1 3.3 us: body(): jnp.einsum('bji,bjk->bik', whole, owned, preferred_element_type=jnp.float32)]
    scatter x1 -> x0, local copies, waits for them, and re-layouts: 4.43 us -> none  [body(): placed = jnp.zeros_like(returned).at[owner_slots].set(returned)]
    all_to_all x6 -> x0, local copies, waits for them, and re-layouts: 3.87 us -> none  [the longest x1 1.88 us: copy_for_each(): return lax.all_to_all(copies, axis, split_axis=0, concat_axis=0, tiled=True)]
  transfers between devices with their start and end apart: 3 -> 0, of which waited for: 2 -> 0; matrix products, arithmetic and copies ran while one was open for 4% -> 0% of each run, Pallas kernels for 0% -> 0%
where the time goes in v1:
time: 98.9 us; the launch traced here: 98.7 us
  Pallas kernels  87.8 us (89%)
  local copies, waits for them, and re-layouts  8.17 us (8%)
  matrix products  1.88 us (2%)
    pallas_call x1, Pallas kernels, body(): pl.pallas_call(functools.partial(kernel, float(blocks * BS * BS)), out_sh...  87.8 us
    unnamed x16, local copies, waits for them, and re-layouts  3.93 us

profile of v1, /device:TPU:1, one launch (start us, length us, event | category | flops | bytes accessed | tf_op | source)
XLA Modules:
  0.0 98.7 jit_solution(17093239007646632596)
XLA Ops:
  0.6 0.0 copy-start
  0.6 0.9 copy-done
  1.6 0.9 fusion.1
  2.5 0.2 copy.16
  2.7 0.2 reshape.24
  2.9 0.8 copy.17.a_hbm
  3.8 87.8 %shard_map.127 = (bf16[64,12,128]{2,1,0:T(8,128)(2,1)}, f32[2,64,768]{2,1,0:T(8,128)}, f32[2,64,768]{2,1,0:T(8,128)}, f32[2,64,768]{2,1,0:T(8,128)}, f32[2,64,768]{2,1,0:T(8,128)}, /*index=5*/f32[8,128]{1,0:T(8,128)}) custom-call(bf16[64,12,128]{2,1,0:T(8,128)(2,1)} %copy.17.a_hbm, bf16[2,768,768]{2,1,0:T(8,128)(2,1)} %ql_hbm.1, ...), custom_call_target="tpu_custom_call" | custom-call | tf_op jit(solution)/shard_map/pallas_call | solution.py:326
  91.6 0.0 copy-start.5
  91.6 0.0 copy-start.4
  91.6 1.2 %slice.11 = f32[1,1]{1,0:T(1,128)} slice(f32[8,128]{1,0:T(8,128)} %get-tuple-element.17), slice={[0:1], [0:1]} | slice | bytes 8 | tf_op jit(solution)/shard_map/slice | solution.py:386
  92.8 0.0 copy-start.3
  92.8 1.2 %fusion.4 = (bf16[64,12,64]{2,1,0:T(8,128)(2,1)S(1)}, bf16[64,12,64]{2,1,0:T(8,128)(2,1)S(1)}) fusion(bf16[64,12,128]{2,1,0:T(8,128)(2,1)} %get-tuple-element.12), kind=kLoop, calls=%fused_computation.6 | loop fusion | bytes 393216 | tf_op jit(solution)/shard_map/slice
  94.1 0.0 copy-start.2
  94.1 0.2 pad_maximum_fusion
  94.2 0.0 copy-start.1
  94.2 0.1 reshape.25
  94.4 0.4 copy.18
  94.8 0.0 copy-done.5
  94.8 0.9 fusion
  95.7 0.0 copy-done.4
  95.7 0.7 copy.23
  96.5 0.0 copy-done.3
  96.5 0.7 copy.24
  97.2 0.0 copy-done.2
  97.2 0.7 copy.25
  98.0 0.0 copy-done.1
  98.0 0.7 copy.26
Async XLA Ops:
  0.6 0.9 copy-start
  91.6 3.2 %copy-start.5 = (s32[128]{0:T(128)S(1)}, s32[128]{0:T(128)}, u32[]{:S(2)}) copy-start(s32[128]{0:T(128)} %param.9) | copy-start | bytes 1540
  91.6 4.1 %copy-start.4 = (f32[2,64,768]{2,1,0:T(8,128)S(1)}, f32[2,64,768]{2,1,0:T(8,128)}, u32[]{:S(2)}) copy-start(f32[2,64,768]{2,1,0:T(8,128)} %get-tuple-element.13) | copy-start | bytes 1179652
  92.8 3.6 %copy-start.3 = (f32[2,64,768]{2,1,0:T(8,128)S(1)}, f32[2,64,768]{2,1,0:T(8,128)}, u32[]{:S(2)}) copy-start(f32[2,64,768]{2,1,0:T(8,128)} %get-tuple-element.14) | copy-start | bytes 1179652
  94.1 3.2 %copy-start.2 = (f32[2,64,768]{2,1,0:T(8,128)S(1)}, f32[2,64,768]{2,1,0:T(8,128)}, u32[]{:S(2)}) copy-start(f32[2,64,768]{2,1,0:T(8,128)} %get-tuple-element.15) | copy-start | bytes 1179652
  94.2 3.7 %copy-start.1 = (f32[2,64,768]{2,1,0:T(8,128)S(1)}, f32[2,64,768]{2,1,0:T(8,128)}, u32[]{:S(2)}) copy-start(f32[2,64,768]{2,1,0:T(8,128)} %get-tuple-element.16) | copy-start | bytes 1179652
